TPU v7x, 32 devices: a whole 2x2x4 slice. The times are simulated.
32 devices in a mesh: trial: 4 (over x, core), north: 2 (over y), east: 4 (over z).
Axes of the slice: x: 2, y: 2, z: 4, core: 2. Of those that a mesh axis runs over, the one named last changes fastest.
Arguments:
- pair_state: bfloat16 [192, 48, 128], P(('trial', 'north'), 'east'), parts along dimension 0, may hold values from -6 to 6
- in_gain: float32 [128], replicated, may hold values from 0.25 to 1.75
- left_weight: bfloat16 [512, 128], P('trial'), parts along dimension 0, may hold values from -0.5 to 0.5
- right_weight: bfloat16 [512, 128], P('trial'), parts along dimension 0, may hold values from -0.5 to 0.5
- left_gate: bfloat16 [512, 128], P('trial'), parts along dimension 0, may hold values from -0.5 to 0.5
- right_gate: bfloat16 [512, 128], P('trial'), parts along dimension 0, may hold values from -0.5 to 0.5
- mid_gain: float32 [128], replicated, may hold values from 0.25 to 1.75
- out_weight: bfloat16 [512, 128], P('trial'), parts along dimension 0, may hold values from -0.5 to 0.5
- out_gate: bfloat16 [512, 128], P('trial'), parts along dimension 0, may hold values from -0.5 to 0.5
Outputs:
- triangle_out: bfloat16 [192, 48, 128], P(('trial', 'north'), 'east'), parts along dimension 0
There are 4 independent parts, one for each index of `trial`. A program takes and returns all parts, laid end to end along the dimension named above; an argument that names none is the same for every part. Nothing has to cross between parts.
All inputs are finite; a program needn't handle non-finite values.
Results may differ from a plain program's by a relative error of at most 0.015.
Values may be sent and summed in bfloat16 or wider, within the bound.
A program may use at most 64 MiB of HBM per device.

v0:
```python
import jax
import jax.numpy as jnp
from jax import lax
from jax.sharding import PartitionSpec as P


def norm_channels(values, channel_gain):
    centred = values - jnp.mean(values, axis=-1, keepdims=True)
    return (
        centred
        * lax.rsqrt(jnp.mean(centred * centred, axis=-1, keepdims=True) + 1e-05)
        * channel_gain
    )


def make_factors(pair_in, in_gain, left_weight, right_weight, left_gate, right_gate):
    ready = norm_channels(pair_in.astype(jnp.float32), in_gain).astype(jnp.bfloat16)
    ready = lax.optimization_barrier(ready)
    left = jnp.einsum("ijc,cd->ijd", ready, left_weight, preferred_element_type=jnp.float32)
    left = left * jax.nn.sigmoid(
        jnp.einsum("ijc,cd->ijd", ready, left_gate, preferred_element_type=jnp.float32)
    )
    right = jnp.einsum("ijc,cd->ijd", ready, right_weight, preferred_element_type=jnp.float32)
    right = right * jax.nn.sigmoid(
        jnp.einsum("ijc,cd->ijd", ready, right_gate, preferred_element_type=jnp.float32)
    )
    return (ready, left.astype(jnp.bfloat16), right.astype(jnp.bfloat16))


def to_pair(mixed, ready, mid_gain, out_weight, out_gate):
    scaled = norm_channels(mixed.astype(jnp.float32), mid_gain).astype(jnp.bfloat16)
    scaled = lax.optimization_barrier(scaled)
    gate = jax.nn.sigmoid(
        jnp.einsum("ijc,cd->ijd", ready, out_gate, preferred_element_type=jnp.float32)
    )
    return (
        jnp.einsum("ijd,dc->ijc", scaled, out_weight, preferred_element_type=jnp.float32) * gate
    ).astype(jnp.bfloat16)


def local(
    pair_state,
    in_gain,
    left_weight,
    right_weight,
    left_gate,
    right_gate,
    mid_gain,
    out_weight,
    out_gate,
):
    ready, left, right = make_factors(
        pair_state, in_gain, left_weight, right_weight, left_gate, right_gate
    )
    count = pair_state.shape[1] * lax.axis_size("east")
    left_lines, right_lines = (
        lax.all_to_all(left, "east", split_axis=2, concat_axis=1, tiled=True),
        lax.all_to_all(right, "east", split_axis=2, concat_axis=1, tiled=True),
    )
    strip = jnp.einsum(
        "ikd,jkd->ijd",
        left_lines,
        lax.all_gather(right_lines, "north", axis=0, tiled=True),
        preferred_element_type=jnp.float32,
    )
    strip = (strip * count ** (-0.5)).astype(jnp.bfloat16)
    mixed = lax.all_to_all(strip, "east", split_axis=1, concat_axis=2, tiled=True)
    return to_pair(mixed, ready, mid_gain, out_weight, out_gate)


def solution(mesh):
    return jax.shard_map(
        local,
        mesh=mesh,
        in_specs=(
            P(("trial", "north"), "east", None),
            P(),
            P("trial", None),
            P("trial", None),
            P("trial", None),
            P("trial", None),
            P(),
            P("trial", None),
            P("trial", None),
        ),
        out_specs=P(("trial", "north"), "east", None),
        check_vma=False,
    )
```

profile of v0, /device:TPU:0, one launch (start us, length us, event | category | flops | bytes accessed | tf_op | source)
XLA Modules:
  0.0 44.6 jit_solution(821063206014544712)
XLA Ops:
  0.0 1.1 %convert_reduce_fusion = f32[24,12]{0,1:T(8,128)S(1)} fusion(bf16[24,12,128]{2,0,1:T(8,128)(2,1)} %param.9), kind=kLoop, calls=%fused_computation.25 | loop fusion | flops 73440 | bytes 74880 | tf_op jit(solution)/shard_map/reduce_sum | solution.py:8
  1.3 0.6 %copy-done.4 = f32[128]{0:T(128)S(1)} copy-done((f32[128]{0:T(128)S(1)}, f32[128]{0:T(128)}, u32[]{:S(2)}) %copy-start.4) | copy-done | bytes 536
  2.3 0.6 %copy-done.6 = bf16[128,128]{1,0:T(8,128)(2,1)S(1)} copy-done((bf16[128,128]{1,0:T(8,128)(2,1)S(1)}, bf16[128,128]{1,0:T(8,128)(2,1)}, u32[]{:S(2)}) %copy-start.6) | copy-done | bytes 32792
  2.9 0.2 fusion.16
  3.1 0.4 copy.34
  3.5 1.1 %reshape.41 = bf16[4,2,4608]{2,1,0:T(2,128)(2,1)} reshape(bf16[128,12,24]{2,1,0:T(8,128)(2,1)S(1)} %bitcast.55) | data formatting | bytes 147456
  4.7 6.5 %all-to-all-start = ((bf16[4,2,4608]{2,1,0:T(2,128)(2,1)}), bf16[4,2,4608]{2,1,0:T(2,128)(2,1)S(1)}, u32[]{:S(2)}, u32[]{:S(2)}) async-start(bf16[4,2,4608]{2,1,0:T(2,128)(2,1)} %reshape.41), calls=%async_computation | async-start | bytes 147456 | tf_op jit(solution)/shard_map/all_to_all | solution.py:58
  11.3 0.6 %copy-done.7 = bf16[128,128]{1,0:T(8,128)(2,1)S(1)} copy-done((bf16[128,128]{1,0:T(8,128)(2,1)S(1)}, bf16[128,128]{1,0:T(8,128)(2,1)}, u32[]{:S(2)}) %copy-start.7) | copy-done | bytes 32792
  11.9 0.2 fusion.15
  12.1 0.4 copy.37
  12.5 1.1 %reshape.43 = bf16[4,2,4608]{2,1,0:T(2,128)(2,1)} reshape(bf16[128,12,24]{2,1,0:T(8,128)(2,1)S(1)} %bitcast.56) | data formatting | bytes 147456
  13.7 3.2 %all-to-all-done = bf16[4,2,4608]{2,1,0:T(2,128)(2,1)S(1)} async-done(((bf16[4,2,4608]{2,1,0:T(2,128)(2,1)}), bf16[4,2,4608]{2,1,0:T(2,128)(2,1)S(1)}, u32[]{:S(2)}, u32[]{:S(2)}) %all-to-all-start) | async-done | bytes 73760 | tf_op jit(solution)/shard_map/all_to_all | solution.py:58
  16.9 3.3 %all-to-all-start.1 = ((bf16[4,2,4608]{2,1,0:T(2,128)(2,1)}), bf16[4,2,4608]{2,1,0:T(2,128)(2,1)S(1)}, u32[]{:S(2)}, u32[]{:S(2)}) async-start(bf16[4,2,4608]{2,1,0:T(2,128)(2,1)} %reshape.43), calls=%async_computation.1 | async-start | bytes 147456 | tf_op jit(solution)/shard_map/all_to_all | solution.py:57
  20.2 0.6 %reshape.42 = bf16[128,12,24]{2,1,0:T(8,128)(2,1)S(1)} reshape(bf16[4,2,4608]{2,1,0:T(2,128)(2,1)S(1)} %all-to-all-done) | data formatting | bytes 147456
  20.8 0.4 copy.35
  21.2 0.3 copy.36
  21.5 6.3 %all_gather.3 = bf16[48,48,32]{1,0,2:T(8,128)(2,1)S(1)} all-gather(bf16[24,48,32]{1,0,2:T(8,128)(2,1)S(1)} %copy.36), channel_id=1, replica_groups=mesh['trial'=4,'north'=2,'east'=4] {'north'}, dimensions={0}, use_global_device_ids=true | all-gather | bytes 221184 | tf_op jit(solution)/shard_map/all_gather | solution.py:63
  27.8 0.6 %reshape.44 = bf16[128,12,24]{2,1,0:T(8,128)(2,1)S(1)} reshape(bf16[4,2,4608]{2,1,0:T(2,128)(2,1)S(1)} %all-to-all-done.1) | data formatting | bytes 147456
  28.4 0.4 copy.38
  28.8 0.3 copy.39
  29.1 0.3 fusion.1
  29.4 0.2 copy.40
  29.6 0.3 reshape.45
  29.9 10.6 %all_to_all.45 = bf16[4,2,4608]{2,1,0:T(2,128)(2,1)S(1)} all-to-all(bf16[4,2,4608]{2,1,0:T(2,128)(2,1)S(1)} %reshape.45), channel_id=1, replica_groups=mesh['trial'=4,'north'=2,'east'=4] {'east'}, dimensions={0} | all-to-all | bytes 147456 | tf_op jit(solution)/shard_map/all_to_all | solution.py:67
  40.5 0.2 reshape.46
  40.9 0.2 multiply_reduce_fusion
  41.2 0.4 copy.41
  41.6 0.3 reshape.32
  41.9 0.4 copy-done.5
  42.4 0.6 %copy-done.3 = bf16[128,128]{1,0:T(8,128)(2,1)S(1)} copy-done((bf16[128,128]{1,0:T(8,128)(2,1)S(1)}, bf16[128,128]{1,0:T(8,128)(2,1)}, u32[]{:S(2)}) %copy-start.3) | copy-done | bytes 32792
  43.2 0.6 %copy-done.8 = bf16[128,128]{1,0:T(8,128)(2,1)S(1)} copy-done((bf16[128,128]{1,0:T(8,128)(2,1)S(1)}, bf16[128,128]{1,0:T(8,128)(2,1)}, u32[]{:S(2)}) %copy-start.8) | copy-done | bytes 32792
  43.7 0.8 %fusion.14 = bf16[24,12,128]{2,0,1:T(8,128)(2,1)} fusion(f32[24,12,128]{2,0,1:T(8,128)S(1)} %fusion.24, bf16[24,12,128]{2,0,1:T(8,128)(2,1)S(1)} %fusion.22, bf16[128,128]{1,0:T(8,128)(2,1)S(1)} %copy-done.8), kind=kOutput, calls=%fused_computation.18 | convolution fusion | flops 9621504 | bytes 327680 | tf_op jit(solution)/shard_map/ijc,cd->ijd/dot_general | solution.py:34
  (25 shorter events, 1.2 us)
Async XLA Ops:
  0.0 2.1 %copy-start = (bf16[128,128]{1,0:T(8,128)(2,1)S(1)}, bf16[128,128]{1,0:T(8,128)(2,1)}, u32[]{:S(2)}) copy-start(bf16[128,128]{1,0:T(8,128)(2,1)} %param.12) | copy-start | bytes 98308
  0.0 1.1 %copy-start.1 = (bf16[24,12,128]{2,0,1:T(8,128)(2,1)S(1)}, bf16[24,12,128]{2,0,1:T(8,128)(2,1)}, u32[]{:S(2)}) copy-start(bf16[24,12,128]{2,0,1:T(8,128)(2,1)} %param.9) | copy-start | bytes 221188
  1.3 0.7 %copy-start.4 = (f32[128]{0:T(128)S(1)}, f32[128]{0:T(128)}, u32[]{:S(2)}) copy-start(f32[128]{0:T(128)} %param.10) | copy-start | bytes 1540
  2.1 0.8 %copy-start.6 = (bf16[128,128]{1,0:T(8,128)(2,1)S(1)}, bf16[128,128]{1,0:T(8,128)(2,1)}, u32[]{:S(2)}) copy-start(bf16[128,128]{1,0:T(8,128)(2,1)} %param.14) | copy-start | bytes 98308
  4.7 6.5 %copy-start.2 = (bf16[128,128]{1,0:T(8,128)(2,1)S(1)}, bf16[128,128]{1,0:T(8,128)(2,1)}, u32[]{:S(2)}) copy-start(bf16[128,128]{1,0:T(8,128)(2,1)} %param.11) | copy-start | bytes 98308
  4.7 12.2 %all-to-all-start = ((bf16[4,2,4608]{2,1,0:T(2,128)(2,1)}), bf16[4,2,4608]{2,1,0:T(2,128)(2,1)S(1)}, u32[]{:S(2)}, u32[]{:S(2)}) async-start(bf16[4,2,4608]{2,1,0:T(2,128)(2,1)} %reshape.41), calls=%async_computation | async-start | bytes 147456 | tf_op jit(solution)/shard_map/all_to_all | solution.py:58
  11.1 0.8 %copy-start.7 = (bf16[128,128]{1,0:T(8,128)(2,1)S(1)}, bf16[128,128]{1,0:T(8,128)(2,1)}, u32[]{:S(2)}) copy-start(bf16[128,128]{1,0:T(8,128)(2,1)} %param.13) | copy-start | bytes 98308
  16.9 10.9 %all-to-all-start.1 = ((bf16[4,2,4608]{2,1,0:T(2,128)(2,1)}), bf16[4,2,4608]{2,1,0:T(2,128)(2,1)S(1)}, u32[]{:S(2)}, u32[]{:S(2)}) async-start(bf16[4,2,4608]{2,1,0:T(2,128)(2,1)} %reshape.43), calls=%async_computation.1 | async-start | bytes 147456 | tf_op jit(solution)/shard_map/all_to_all | solution.py:57
  41.6 0.7 %copy-start.5 = (f32[128]{0:T(128)S(1)}, f32[128]{0:T(128)}, u32[]{:S(2)}) copy-start(f32[128]{0:T(128)} %param.15) | copy-start | bytes 1540
  42.2 0.8 %copy-start.3 = (bf16[128,128]{1,0:T(8,128)(2,1)S(1)}, bf16[128,128]{1,0:T(8,128)(2,1)}, u32[]{:S(2)}) copy-start(bf16[128,128]{1,0:T(8,128)(2,1)} %param.16) | copy-start | bytes 98308
  43.0 0.8 %copy-start.8 = (bf16[128,128]{1,0:T(8,128)(2,1)S(1)}, bf16[128,128]{1,0:T(8,128)(2,1)}, u32[]{:S(2)}) copy-start(bf16[128,128]{1,0:T(8,128)(2,1)} %param.17) | copy-start | bytes 98308
where the time goes:
time: 45.3 us; the launch traced here: 44.6 us
  blocking collectives  17 us (38%)
  local copies, waits for them, and re-layouts  10.4 us (23%)
  starting transfers between devices  9.77 us (22%)
  waiting for transfers between devices  3.24 us (7%)
  matrix products  2.02 us (4%)
  other arithmetic  1.96 us (4%)
    all_to_all x1, blocking collectives, local(): lax.all_to_all(strip, 'east', split_axis=1, concat_axis=2, tiled=True)  10.6 us
    unnamed x24, local copies, waits for them, and re-layouts  7.31 us
    all_to_all x1, starting transfers between devices, local(): lax.all_to_all(right, 'east', split_axis=2, concat_axis=1, tiled=True)  6.48 us
    all_gather x1, blocking collectives, local(): lax.all_gather(right_lines, 'north', axis=0, tiled=True)  6.34 us
    all_to_all x1, starting transfers between devices, local(): lax.all_to_all(left, 'east', split_axis=2, concat_axis=1, tiled=True)  3.29 us
    all_to_all x1, waiting for transfers between devices, local(): lax.all_to_all(right, 'east', split_axis=2, concat_axis=1, tiled=True)  3.23 us
    reduce_sum x2, other arithmetic, norm_channels(): centred = values - jnp.mean(values, axis=-1, keepdims=True)  1.19 us
  transfers between devices with their start and end apart: 2, of which 1 were waited for; matrix products, arithmetic and copies ran while one was open for 7% of the time, Pallas kernels for 0%

commit v1 on v0

v1 whole, which is shorter than its diff:
```python
import functools
import math

import jax
import jax.numpy as jnp
from jax import lax
from jax.experimental import pallas as pl
from jax.experimental.pallas import tpu as pltpu
from jax.sharding import PartitionSpec as P

MESH = pl.DeviceIdType.MESH


def norm_channels(values, gain):
    centred = values - jnp.mean(values, axis=-1, keepdims=True)
    return centred * lax.rsqrt(jnp.mean(centred * centred, axis=-1, keepdims=True) + 1e-05) * gain


def logistic(values):
    return 0.5 * jnp.tanh(0.5 * values) + 0.5


def dot(a, b):
    return jnp.dot(a, b, preferred_element_type=jnp.float32)


def tile_of(size, step, most):
    return max(t for t in range(step, most + 1, step) if size % t == 0)


def loop(count, body):
    if count == 1:
        body(0)
    else:
        pl.loop(0, count)(body)


def kernel(
    sizes,
    x_hbm, in_gain_hbm, lw_hbm, rw_hbm, lg_hbm, rg_hbm, mid_gain_hbm, ow_hbm, og_hbm,
    out_ref,
    xs, in_gain, lw, rw, lg, rg, mid_gain, ow, og,
    left, right, gate, sent, got,
    load_sem, pair_send, pair_recv, tile_send, tile_recv,
):
    N, E, R, C, IT, JT = sizes
    rows = R * C
    block = IT * JT
    n = lax.axis_index("north")
    e = lax.axis_index("east")

    barrier = pltpu.get_barrier_semaphore()
    for d in range(1, N):
        pl.semaphore_signal(barrier, inc=1, device_id={"north": lax.rem(n + d, N)}, device_id_type=MESH)
    for d in range(1, E):
        pl.semaphore_signal(barrier, inc=1, device_id={"east": lax.rem(e + d, E)}, device_id_type=MESH)

    loads = [pltpu.make_async_copy(x_hbm, xs.at[n], load_sem.at[0])]
    for at, (src, dst) in enumerate(
        (
            (in_gain_hbm, in_gain), (lw_hbm, lw), (lg_hbm, lg), (rw_hbm, rw),
            (rg_hbm, rg), (og_hbm, og), (mid_gain_hbm, mid_gain), (ow_hbm, ow),
        )
    ):
        loads.append(pltpu.make_async_copy(src, dst, load_sem.at[at + 1]))
    for load in loads:
        load.start()
    loads[0].wait()
    pl.semaphore_wait(barrier, N - 1 + E - 1)

    pair_copies = []
    for d in range(1, N):
        pair_copies.append(
            pltpu.make_async_remote_copy(
                xs.at[n], xs.at[n], pair_send.at[d], pair_recv.at[d],
                device_id={"north": lax.rem(n + d, N)}, device_id_type=MESH,
            )
        )
        pair_copies[-1].start()
    for load in loads[1:]:
        load.wait()

    def ready_rows(m, start):
        values = xs[m, pl.ds(start, block), :].astype(jnp.float32)
        return norm_channels(values, in_gain[...]).astype(jnp.bfloat16)

    def own(at):
        start = pl.multiple_of(at * block, block)
        ready = ready_rows(n, start)
        at_rows = pl.ds(start, block)
        left[at_rows, :] = dot(ready, lw[...]) * logistic(dot(ready, lg[...]))
        right[n, at_rows, :] = dot(ready, rw[...]) * logistic(dot(ready, rg[...]))
        gate[at_rows, :] = logistic(dot(ready, og[...]))

    loop(rows // block, own)

    def other(m):
        def body(at):
            start = pl.multiple_of(at * block, block)
            ready = ready_rows(m, start)
            right[m, pl.ds(start, block), :] = dot(ready, rw[...]) * logistic(dot(ready, rg[...]))

        loop(rows // block, body)

    def tile(slot, target):
        def one(at):
            it, jt = at // (C // JT), lax.rem(at, C // JT)
            first = target * C + jt * JT
            m, j = first // R, lax.rem(first, R)

            def step(k, sums):
                lines = left[pl.ds(pl.multiple_of(k * R + it * IT, 8), IT), :]
                return tuple(
                    sums[a] + lines * right[m, pl.ds(k * R + j + a, 1), :] for a in range(JT)
                )

            sums = lax.fori_loop(
                0, C, step, tuple(jnp.zeros((IT, left.shape[1]), jnp.float32) for _ in range(JT))
            )
            start = pl.multiple_of(at * block, block)
            sent[slot, pl.ds(start, block), :] = jnp.concatenate(sums, axis=0).astype(jnp.bfloat16)

        loop(rows // block, one)

    def tile_copy(slot, peer, landing):
        return pltpu.make_async_remote_copy(
            sent.at[slot], got.at[landing], tile_send.at[slot], tile_recv.at[landing],
            device_id={"east": peer}, device_id_type=MESH,
        )

    reach = R // C
    for s in range(E):
        if s == min(reach, E - 1):
            for d in range(1, N):
                m = lax.rem(n + N - d, N)
                pltpu.make_async_remote_copy(
                    xs.at[m], xs.at[m], pair_send.at[d], pair_recv.at[d],
                    device_id={"north": m}, device_id_type=MESH,
                ).wait_recv()
                other(m)
        target = lax.rem(n * reach + s, E)
        tile(s, target)

        @pl.when(target != e)
        def _():
            tile_copy(s, target, e).start()

    self_slot = lax.rem(e + N * E - n * reach, E)
    for d in range(1, E):
        peer = lax.rem(e + d, E)
        tile_copy(0, peer, peer).wait_recv()

    def finish(at):
        start = pl.multiple_of(at * block, block)
        total = sent[self_slot, pl.ds(start, block), :].astype(jnp.float32)
        for d in range(1, E):
            total += got[lax.rem(e + d, E), pl.ds(start, block), :].astype(jnp.float32)
        mixed = (total * (C * E) ** (-0.5)).astype(jnp.bfloat16).astype(jnp.float32)
        scaled = norm_channels(mixed, mid_gain[...]).astype(jnp.bfloat16)
        it, jt = at // (C // JT), at % (C // JT)
        gates = jnp.concatenate(
            [gate[pl.ds(pl.multiple_of((jt * JT + a) * R + it * IT, 8), IT), :] for a in range(JT)],
            axis=0,
        )
        out_ref[pl.ds(start, block), :] = (dot(scaled, ow[...]) * gates).astype(jnp.bfloat16)

    loop(rows // block, finish)

    for s in range(E):
        @pl.when(lax.rem(n * reach + s, E) != e)
        def _():
            tile_copy(s, lax.rem(n * reach + s, E), e).wait_send()
    for copy in pair_copies:
        copy.wait_send()


def local(N, E, pair_state, in_gain, lw, rw, lg, rg, mid_gain, ow, og):
    R, C, width = pair_state.shape
    mix = lw.shape[1]
    IT = tile_of(R, 8, 24)
    JT = tile_of(math.gcd(R, C), 1, 12)
    rows = R * C
    x = pair_state.transpose(1, 0, 2).reshape(rows, width)
    f32, bf16 = jnp.float32, jnp.bfloat16
    any_space = pl.BlockSpec(memory_space=pl.ANY)
    out = pl.pallas_call(
        functools.partial(kernel, (N, E, R, C, IT, JT)),
        out_shape=jax.ShapeDtypeStruct((rows, width), bf16),
        in_specs=[any_space] * 9,
        out_specs=pl.BlockSpec(memory_space=pltpu.VMEM),
        scratch_shapes=[
            pltpu.VMEM((N, rows, width), bf16),
            pltpu.VMEM((1, width), f32),
            pltpu.VMEM((width, mix), bf16),
            pltpu.VMEM((width, mix), bf16),
            pltpu.VMEM((width, mix), bf16),
            pltpu.VMEM((width, mix), bf16),
            pltpu.VMEM((1, mix), f32),
            pltpu.VMEM((mix, width), bf16),
            pltpu.VMEM((width, width), bf16),
            pltpu.VMEM((rows, mix), f32),
            pltpu.VMEM((N, rows, mix), f32),
            pltpu.VMEM((rows, width), f32),
            pltpu.VMEM((E, rows, mix), bf16),
            pltpu.VMEM((E, rows, mix), bf16),
            pltpu.SemaphoreType.DMA((9,)),
            pltpu.SemaphoreType.DMA((N,)),
            pltpu.SemaphoreType.DMA((N,)),
            pltpu.SemaphoreType.DMA((E,)),
            pltpu.SemaphoreType.DMA((E,)),
        ],
        compiler_params=pltpu.CompilerParams(collective_id=0, has_side_effects=True),
    )(x, in_gain[None], lw, rw, lg, rg, mid_gain[None], ow, og)
    out = out.reshape(R // IT, C, IT, width).transpose(0, 2, 1, 3)
    return out.reshape(R, C, width)


def solution(mesh):
    weight = P("trial", None)
    return jax.shard_map(
        functools.partial(local, mesh.shape["north"], mesh.shape["east"]),
        mesh=mesh,
        in_specs=(
            P(("trial", "north"), "east", None),
            P(), weight, weight, weight, weight, P(), weight, weight,
        ),
        out_specs=P(("trial", "north"), "east", None),
        check_vma=False,
    )
```

time: 45.3 us -> 16.1 us (0.36)
  the two profiles are of different devices: /device:TPU:0 before, /device:TPU:24 now
where the time goes in v1:
time: 16.1 us; the launch traced here: 15.9 us
  Pallas kernels  14.4 us (89%)
  local copies, waits for them, and re-layouts  1.52 us (9%)
    pallas_call x1, Pallas kernels, local(): pl.pallas_call(functools.partial(kernel, (N, E, R, C, IT, JT)), out_shape...  14.4 us
    unnamed x1, local copies, waits for them, and re-layouts  1.52 us

profile of v1, /device:TPU:24, one launch (start us, length us, event | category | flops | bytes accessed | tf_op | source)
XLA Modules:
  0.0 15.9 jit_solution(9141261301485116440)
XLA Ops:
  0.0 14.4 %shard_map.91 = bf16[288,128]{1,0:T(8,128)(2,1)} custom-call(bf16[288,128]{1,0:T(8,128)(2,1)} %bitcast.11, f32[1,128]{1,0:T(1,128)} %bitcast.12, bf16[128,128]{1,0:T(8,128)(2,1)} %lw_hbm.1, bf16[128,128]{1,0:T(8,128)(2,1)} %rw_hbm.1, bf16[128,128]{1,0:T(8,128)(2,1)} %lg_hbm.1, bf16[128,128]{1,0:T(8,128)(2,1)} %rg_hbm.1, f32[1,128]{1,0:T(1,128)} %bitcast.13, ...), custom_call_target="tpu_custom_call" | custom-call | tf_op jit(solution)/shard_map/pallas_call | solution.py:186
  14.4 1.5 %copy.11 = bf16[24,12,128]{2,0,1:T(8,128)(2,1)} copy(bf16[24,12,128]{2,0,1:T(8,128)(2,1)} %bitcast.10) | data formatting | bytes 147456

commit v2 on v1

v2 whole, which is shorter than its diff:
```python
import functools
import math

import jax
import jax.numpy as jnp
from jax import lax
from jax.experimental import pallas as pl
from jax.experimental.pallas import tpu as pltpu
from jax.sharding import PartitionSpec as P

MESH = pl.DeviceIdType.MESH


def norm_channels(values, gain):
    centred = values - jnp.mean(values, axis=-1, keepdims=True)
    return centred * lax.rsqrt(jnp.mean(centred * centred, axis=-1, keepdims=True) + 1e-05) * gain


def logistic(values):
    return 0.5 * jnp.tanh(0.5 * values) + 0.5


def dot(a, b):
    return jnp.dot(a, b, preferred_element_type=jnp.float32)


def tile_of(size, step, most):
    return max(t for t in range(step, most + 1, step) if size % t == 0)


def loop(count, body):
    if count == 1:
        body(0)
    else:
        pl.loop(0, count)(body)


def kernel(
    sizes,
    x_hbm, in_gain_hbm, lw_hbm, rw_hbm, lg_hbm, rg_hbm, mid_gain_hbm, ow_hbm, og_hbm,
    out_ref,
    x, in_gain, lw, rw, lg, rg, mid_gain, ow, og,
    left, right, gate, total, packed, lines, pieces, sent, got, right_sent, right_got,
    load_sem, sent_sem, got_sem, right_sent_sem, right_got_sem,
):
    N, E, R, C, IT, JT = sizes
    S = min(R, C)
    T = R // C
    rows = R * C
    block = IT * JT
    n = lax.axis_index("north")
    e = lax.axis_index("east")

    barrier = pltpu.get_barrier_semaphore()
    for far in reversed(range(1, N * E)):
        pl.semaphore_signal(
            barrier, inc=1,
            device_id={"north": lax.rem(n + far // E, N), "east": lax.rem(e + far % E, E)},
            device_id_type=MESH,
        )

    loads = [
        pltpu.make_async_copy(src, dst, load_sem.at[at])
        for at, (src, dst) in enumerate(
            (
                (x_hbm, x), (in_gain_hbm, in_gain), (lw_hbm, lw), (lg_hbm, lg), (rw_hbm, rw),
                (rg_hbm, rg), (og_hbm, og), (mid_gain_hbm, mid_gain), (ow_hbm, ow),
            )
        )
    ]
    for load in loads:
        load.start()
    for load in loads:
        load.wait()

    def own(at):
        at_rows = pl.ds(pl.multiple_of(at * block, block), block)
        ready = norm_channels(x[at_rows, :].astype(jnp.float32), in_gain[...]).astype(jnp.bfloat16)
        left[at_rows, :] = dot(ready, lw[...]) * logistic(dot(ready, lg[...]))
        right[at_rows, :] = dot(ready, rw[...]) * logistic(dot(ready, rg[...]))
        gate[at_rows, :] = logistic(dot(ready, og[...]))
        sent[T, at_rows, :] = left[at_rows, :].astype(jnp.bfloat16)
        if S == R:
            right_sent[0, at_rows, :] = right[at_rows, :].astype(jnp.bfloat16)

    loop(rows // block, own)

    if S < R:
        for t in range(T):
            for k in range(C):
                packed[pl.ds(k * S, S), :] = right[pl.ds(k * R + t * S, S), :]
            right_sent[t] = packed[...].astype(jnp.bfloat16)

    def sums_of(left_ref, i, right_ref, stride, j):
        def step(k, sums):
            lanes = left_ref[pl.ds(pl.multiple_of(k * R + i, 8), IT), :]
            return tuple(
                sums[a] + lanes * right_ref[pl.ds(k * stride + j + a, 1), :] for a in range(JT)
            )

        zeros = jnp.zeros((IT, left_ref.shape[1]), jnp.float32)
        return jnp.concatenate(lax.fori_loop(0, C, step, (zeros,) * JT, unroll=2), axis=0)

    for t in range(T):
        def tile(at):
            it, jt = at // (C // JT), at % (C // JT)
            at_rows = pl.ds(pl.multiple_of(at * block, block), block)
            sums = sums_of(left, it * IT, right, R, t * C + jt * JT)

            @pl.when(n * T + t == e)
            def _():
                total[at_rows, :] = sums

            sent[t, at_rows, :] = sums.astype(jnp.bfloat16)

        loop(rows // block, tile)

    pl.semaphore_wait(barrier, N * E - 1)

    def right_copy(t, p, target_north, target_east, source_east):
        return pltpu.make_async_remote_copy(
            right_sent.at[t], right_got.at[p, source_east],
            right_sent_sem.at[t, lax.rem(target_north + N - n, N)], right_got_sem.at[p, source_east],
            device_id={"north": target_north, "east": target_east}, device_id_type=MESH,
        )

    def right_copies(act):
        for t in range(R // S):
            piece = n * (R // S) + t
            target, p = piece // (C // S), lax.rem(piece, C // S)
            for d in reversed(range(1, N)):
                act(right_copy(t, p, lax.rem(n + d, N), target, e))
            if T == 0:
                @pl.when(target != e)
                def _():
                    act(right_copy(t, p, n, target, e))

    def got_copy(slot, peer, source):
        return pltpu.make_async_remote_copy(
            sent.at[slot], got.at[source], sent_sem.at[peer], got_sem.at[source],
            device_id={"east": peer}, device_id_type=MESH,
        )

    def got_copies(act):
        for d in range(1, E):
            peer = lax.rem(e + d, E)
            slot = T
            if T:
                slot = jnp.where(peer // T == n, lax.rem(peer, T), T)
            act(got_copy(slot, peer, e))

    right_copies(lambda copy: copy.start())
    got_copies(lambda copy: copy.start())

    order = [sorted(range(E), key=lambda s: (abs(s - v), s)) for v in range(E)]
    sources = [sum(jnp.where(e == v, order[v][d], 0) for v in range(E)) for d in range(E)]

    def add_tiles():
        for source in sources[1:]:
            got_copy(T, source, source).wait_recv()

            def add(at):
                at_rows = pl.ds(pl.multiple_of(at * block, block), block)
                total[at_rows, :] += got[source, at_rows, :].astype(jnp.float32)

            loop(rows // block, add)

    def multiply_lines():
        for d, source in enumerate(sources):
            if d:
                got_copy(T, source, source).wait_recv()

                def widen(at):
                    at_rows = pl.ds(pl.multiple_of(at * block, block), block)
                    lines[at_rows, :] = got[source, at_rows, :].astype(jnp.float32)

                loop(rows // block, widen)
            for p in range(C // S):
                owner = (e * (C // S) + p) // (R // S)

                def widen_piece(ref):
                    def widen(at):
                        at_rows = pl.ds(pl.multiple_of(at * C * JT, C * JT), C * JT)
                        pieces[at_rows, :] = ref[at_rows, :].astype(jnp.float32)

                    loop(S // JT, widen)

                if d == 0 and T == 0:
                    @pl.when(owner == n)
                    def _():
                        widen_piece(right_sent.at[0])

                    @pl.when(owner != n)
                    def _():
                        right_copy(0, p, owner, e, source).wait_recv()
                        widen_piece(right_got.at[p, source])
                else:
                    right_copy(0, p, owner, e, source).wait_recv()
                    widen_piece(right_got.at[p, source])

                def multiply(at):
                    it, jt = at // (S // JT), at % (S // JT)
                    to = it * (C // JT) + p * (S // JT) + jt
                    at_rows = pl.ds(pl.multiple_of(to * block, block), block)
                    sums = sums_of(left if d == 0 else lines, it * IT, pieces, S, jt * JT)
                    if d:
                        sums += total[at_rows, :]
                    total[at_rows, :] = sums

                loop((R // IT) * (S // JT), multiply)

    if T:
        pl.when(e // T == n)(add_tiles)
        pl.when(e // T != n)(multiply_lines)
    else:
        multiply_lines()

    def finish(at):
        start = pl.multiple_of(at * block, block)
        mixed = (total[pl.ds(start, block), :] * (C * E) ** (-0.5)).astype(jnp.bfloat16)
        scaled = norm_channels(mixed.astype(jnp.float32), mid_gain[...]).astype(jnp.bfloat16)
        it, jt = at // (C // JT), at % (C // JT)
        gates = jnp.concatenate(
            [gate[pl.ds(pl.multiple_of((jt * JT + a) * R + it * IT, 8), IT), :] for a in range(JT)],
            axis=0,
        )
        out_ref[pl.ds(start, block), :] = (dot(scaled, ow[...]) * gates).astype(jnp.bfloat16)

    loop(rows // block, finish)
    right_copies(lambda copy: copy.wait_send())
    got_copies(lambda copy: copy.wait_send())


def local(N, E, pair_state, in_gain, lw, rw, lg, rg, mid_gain, ow, og):
    R, C, width = pair_state.shape
    mix = lw.shape[1]
    S, T = min(R, C), R // C
    IT = tile_of(R, 8, 24)
    JT = tile_of(math.gcd(R, C), 1, 12)
    rows = R * C
    x = pair_state.transpose(1, 0, 2).reshape(rows, width)
    f32, bf16 = jnp.float32, jnp.bfloat16
    dma = pltpu.SemaphoreType.DMA
    out = pl.pallas_call(
        functools.partial(kernel, (N, E, R, C, IT, JT)),
        out_shape=pltpu.VMEM((rows, width), bf16),
        in_specs=[pl.BlockSpec(memory_space=pl.ANY)] * 9,
        out_specs=pl.BlockSpec(memory_space=pltpu.VMEM),
        scratch_shapes=[
            pltpu.VMEM((rows, width), bf16),
            pltpu.VMEM((1, width), f32),
            pltpu.VMEM((width, mix), bf16),
            pltpu.VMEM((width, mix), bf16),
            pltpu.VMEM((width, mix), bf16),
            pltpu.VMEM((width, mix), bf16),
            pltpu.VMEM((1, mix), f32),
            pltpu.VMEM((mix, width), bf16),
            pltpu.VMEM((width, width), bf16),
            pltpu.VMEM((rows, mix), f32),
            pltpu.VMEM((rows, mix), f32),
            pltpu.VMEM((rows, width), f32),
            pltpu.VMEM((rows, mix), f32),
            pltpu.VMEM((C * S, mix), f32),
            pltpu.VMEM((rows, mix), f32),
            pltpu.VMEM((C * S, mix), f32),
            pltpu.VMEM((T + 1, rows, mix), bf16),
            pltpu.VMEM((E, rows, mix), bf16),
            pltpu.VMEM((R // S, C * S, mix), bf16),
            pltpu.VMEM((C // S, E, C * S, mix), bf16),
            dma((9,)),
            dma((E,)),
            dma((E,)),
            dma((R // S, N)),
            dma((C // S, E)),
        ],
        compiler_params=pltpu.CompilerParams(collective_id=0, has_side_effects=True),
    )(x, in_gain[None], lw, rw, lg, rg, mid_gain[None], ow, og)
    out = out.reshape(R // IT, C, IT, width).transpose(0, 2, 1, 3)
    return out.reshape(R, C, width)


def solution(mesh):
    weight = P("trial", None)
    return jax.shard_map(
        functools.partial(local, mesh.shape["north"], mesh.shape["east"]),
        mesh=mesh,
        in_specs=(
            P(("trial", "north"), "east", None),
            P(), weight, weight, weight, weight, P(), weight, weight,
        ),
        out_specs=P(("trial", "north"), "east", None),
        check_vma=False,
    )
```

time: 16.1 us -> 16.9 us (1.050)
  the two profiles are of different devices: /device:TPU:24 before, /device:TPU:0 now
where the time goes in v2:
time: 16.9 us; the launch traced here: 16.7 us
  Pallas kernels  16.1 us (95%)
  local copies, waits for them, and re-layouts  0.64 us (4%)
    pallas_call x1, Pallas kernels, local(): pl.pallas_call(functools.partial(kernel, (N, E, R, C, IT, JT)), out_shape...  16.1 us
    unnamed x1, local copies, waits for them, and re-layouts  0.64 us

profile of v2, /device:TPU:0, one launch (start us, length us, event | category | flops | bytes accessed | tf_op | source)
XLA Modules:
  0.0 16.7 jit_solution(13040333011543153687)
XLA Ops:
  0.0 16.1 %shard_map.91 = bf16[288,128]{1,0:T(8,128)(2,1)S(1)} custom-call(bf16[288,128]{1,0:T(8,128)(2,1)} %bitcast.11, f32[1,128]{1,0:T(1,128)} %bitcast.12, bf16[128,128]{1,0:T(8,128)(2,1)} %lw_hbm.1, bf16[128,128]{1,0:T(8,128)(2,1)} %rw_hbm.1, bf16[128,128]{1,0:T(8,128)(2,1)} %lg_hbm.1, bf16[128,128]{1,0:T(8,128)(2,1)} %rg_hbm.1, f32[1,128]{1,0:T(1,128)} %bitcast.13, ...), custom_call_target="tpu_custom_call" | custom-call | tf_op jit(solution)/shard_map/pallas_call | solution.py:244
  16.1 0.6 %copy.11 = bf16[24,12,128]{2,0,1:T(8,128)(2,1)} copy(bf16[24,12,128]{2,0,1:T(8,128)(2,1)S(1)} %bitcast.10) | data formatting | bytes 147456

commit v3 on v2

v3 whole, which is shorter than its diff:
```python
import functools
import math

import jax
import jax.numpy as jnp
from jax import lax
from jax.experimental import pallas as pl
from jax.experimental.pallas import tpu as pltpu
from jax.sharding import PartitionSpec as P

MESH = pl.DeviceIdType.MESH


def norm_channels(values, gain):
    centred = values - jnp.mean(values, axis=-1, keepdims=True)
    return centred * lax.rsqrt(jnp.mean(centred * centred, axis=-1, keepdims=True) + 1e-05) * gain


def logistic(values):
    return 0.5 * jnp.tanh(0.5 * values) + 0.5


def dot(a, b):
    return jnp.dot(a, b, preferred_element_type=jnp.float32)


def tile_of(size, step, most):
    return max(t for t in range(step, most + 1, step) if size % t == 0)


def loop(count, body):
    if count == 1:
        body(0)
    else:
        pl.loop(0, count)(body)


def kernel(
    sizes,
    x_hbm, in_gain_hbm, lw_hbm, rw_hbm, lg_hbm, rg_hbm, mid_gain_hbm, ow_hbm, og_hbm,
    out_ref,
    x, in_gain, lw, rw, lg, rg, mid_gain, ow, og,
    left, right, gate, packed, pieces, sent, got, right_sent, right_got,
    load_sem, sent_sem, got_sem, right_sent_sem, right_got_sem, below_sem, above_sem,
):
    N, E, R, C, IT, JT = sizes
    S = min(R, C)
    T, parts = R // S, C // S
    rows, piece_rows, block = R * C, R * S, IT * JT
    n = lax.axis_index("north")
    e = lax.axis_index("east")
    below, above = lax.max(e - 1, 0), lax.min(e + 1, E - 1)
    has_below, has_above = e > 0, e < E - 1

    def signal(sem, axis, peer):
        pl.semaphore_signal(sem, inc=1, device_id={axis: peer}, device_id_type=MESH)

    barrier = pltpu.get_barrier_semaphore()
    for d in range(1, N):
        signal(barrier, "north", lax.rem(n + d, N))
    pl.when(has_below)(lambda: signal(barrier, "east", below))
    pl.when(has_above)(lambda: signal(barrier, "east", above))

    loads = [
        pltpu.make_async_copy(src, dst, load_sem.at[at])
        for at, (src, dst) in enumerate(
            (
                (x_hbm, x), (in_gain_hbm, in_gain), (lw_hbm, lw), (lg_hbm, lg), (rw_hbm, rw),
                (rg_hbm, rg), (og_hbm, og), (mid_gain_hbm, mid_gain), (ow_hbm, ow),
            )
        )
    ]
    for load in loads:
        load.start()
    for load in loads:
        load.wait()

    def own(at):
        at_rows = pl.ds(pl.multiple_of(at * block, block), block)
        ready = norm_channels(x[at_rows, :].astype(jnp.float32), in_gain[...]).astype(jnp.bfloat16)
        right[at_rows, :] = dot(ready, rw[...]) * logistic(dot(ready, rg[...]))
        left[at_rows, :] = dot(ready, lw[...]) * logistic(dot(ready, lg[...]))
        gate[at_rows, :] = logistic(dot(ready, og[...]))
        if S == R:
            right_sent[0, at_rows, :] = right[at_rows, :].astype(jnp.bfloat16)

    loop(rows // block, own)

    if S < R:
        for t in range(T):
            for k in range(C):
                packed[pl.ds(k * S, S), :] = right[pl.ds(k * R + t * S, S), :]
            right_sent[t] = packed[...].astype(jnp.bfloat16)

    pl.semaphore_wait(
        barrier, N - 1 + has_below.astype(jnp.int32) + has_above.astype(jnp.int32)
    )

    def right_copy(d, t, peer, owner):
        return pltpu.make_async_remote_copy(
            right_sent.at[t], right_got.at[owner, t],
            right_sent_sem.at[d, t], right_got_sem.at[owner, t],
            device_id={"north": peer}, device_id_type=MESH,
        )

    def right_copies(act):
        for d in range(1, N):
            for t in range(T):
                act(right_copy(d, t, lax.rem(n + d, N), n))

    right_copies(lambda copy: copy.start())

    @pl.when(has_below & has_above)
    def _():
        signal(below_sem, "east", above)
        signal(above_sem, "east", below)

    def tile(m, t, right_ref, stride, offset):
        def one(at):
            it, jt = at // (S // JT), at % (S // JT)

            def step(k, sums):
                lanes = left[pl.ds(pl.multiple_of(k * R + it * IT, 8), IT), :]
                first = k * stride + offset + jt * JT
                return tuple(sums[a] + lanes * right_ref[pl.ds(first + a, 1), :] for a in range(JT))

            zeros = jnp.zeros((IT, left.shape[1]), jnp.float32)
            sums = lax.fori_loop(0, C, step, (zeros,) * JT, unroll=2)
            at_rows = pl.ds(pl.multiple_of(at * block, block), block)
            sent[m, t, at_rows, :] = jnp.concatenate(sums, axis=0).astype(jnp.bfloat16)

        loop(piece_rows // block, one)

    for t in range(T):
        tile(n, t, right, R, t * S)

    for k in range(2, E):
        @pl.when(e - k >= 0)
        def _():
            pl.semaphore_wait(below_sem, 1)
            pl.when(has_above)(lambda: signal(below_sem, "east", above))

        @pl.when(e + k < E)
        def _():
            pl.semaphore_wait(above_sem, 1)
            pl.when(has_below)(lambda: signal(above_sem, "east", below))

    def got_copy(m, t, peer, source, p):
        return pltpu.make_async_remote_copy(
            sent.at[m, t], got.at[source, p], sent_sem.at[m, t], got_sem.at[source, p],
            device_id={"east": peer}, device_id_type=MESH,
        )

    def send(m, act):
        for t in range(T):
            target, p = (m * T + t) // parts, lax.rem(m * T + t, parts)

            @pl.when(target != e)
            def _():
                act(got_copy(m, t, target, e, p))

    send(n, lambda copy: copy.start())

    for d in range(1, N):
        m = lax.rem(n + N - d, N)
        for t in range(T):
            right_copy(d, t, m, m).wait_recv()

            def widen(at):
                at_rows = pl.ds(pl.multiple_of(at * C * JT, C * JT), C * JT)
                pieces[at_rows, :] = right_got[m, t, at_rows, :].astype(jnp.float32)

            loop(S // JT, widen)
            tile(m, t, pieces, S, 0)
            target, p = (m * T + t) // parts, lax.rem(m * T + t, parts)

            @pl.when(target != e)
            def _():
                got_copy(m, t, target, e, p).start()

    for d in range(1, E):
        source = lax.rem(e + d, E)
        for p in range(parts):
            got_copy(0, 0, source, source, p).wait_recv()

    for p in range(parts):
        piece = e * parts + p
        own_north, own_piece = piece // T, lax.rem(piece, T)

        def finish(at):
            at_rows = pl.ds(pl.multiple_of(at * block, block), block)
            total = sent[own_north, own_piece, at_rows, :].astype(jnp.float32)
            for d in range(1, E):
                total += got[lax.rem(e + d, E), p, at_rows, :].astype(jnp.float32)
            mixed = (total * (C * E) ** (-0.5)).astype(jnp.bfloat16)
            scaled = norm_channels(mixed.astype(jnp.float32), mid_gain[...]).astype(jnp.bfloat16)
            it, jt = at // (S // JT), at % (S // JT)
            first = (p * S + jt * JT) * R + it * IT
            gates = jnp.concatenate(
                [gate[pl.ds(pl.multiple_of(first + a * R, 8), IT), :] for a in range(JT)], axis=0
            )
            out_rows = pl.ds(pl.multiple_of(p * piece_rows + at * block, block), block)
            out_ref[out_rows, :] = (dot(scaled, ow[...]) * gates).astype(jnp.bfloat16)

        loop(piece_rows // block, finish)

    right_copies(lambda copy: copy.wait_send())
    for m in range(N):
        send(lax.rem(n + m, N), lambda copy: copy.wait_send())


def local(N, E, pair_state, in_gain, lw, rw, lg, rg, mid_gain, ow, og):
    R, C, width = pair_state.shape
    mix = lw.shape[1]
    S = min(R, C)
    T, parts = R // S, C // S
    IT = tile_of(R, 8, 24)
    JT = tile_of(math.gcd(R, C), 1, 12)
    rows = R * C
    x = pair_state.transpose(1, 0, 2).reshape(rows, width)
    f32, bf16 = jnp.float32, jnp.bfloat16
    dma = pltpu.SemaphoreType.DMA
    out = pl.pallas_call(
        functools.partial(kernel, (N, E, R, C, IT, JT)),
        out_shape=pltpu.VMEM((rows, width), bf16),
        in_specs=[pl.BlockSpec(memory_space=pl.ANY)] * 9,
        out_specs=pl.BlockSpec(memory_space=pltpu.VMEM),
        scratch_shapes=[
            pltpu.VMEM((rows, width), bf16),
            pltpu.VMEM((1, width), f32),
            pltpu.VMEM((width, mix), bf16),
            pltpu.VMEM((width, mix), bf16),
            pltpu.VMEM((width, mix), bf16),
            pltpu.VMEM((width, mix), bf16),
            pltpu.VMEM((1, mix), f32),
            pltpu.VMEM((mix, width), bf16),
            pltpu.VMEM((width, width), bf16),
            pltpu.VMEM((rows, mix), f32),
            pltpu.VMEM((rows, mix), f32),
            pltpu.VMEM((rows, width), f32),
            pltpu.VMEM((C * S, mix), f32),
            pltpu.VMEM((C * S, mix), f32),
            pltpu.VMEM((N, T, R * S, mix), bf16),
            pltpu.VMEM((E, parts, R * S, mix), bf16),
            pltpu.VMEM((T, C * S, mix), bf16),
            pltpu.VMEM((N, T, C * S, mix), bf16),
            dma((9,)),
            dma((N, T)),
            dma((E, parts)),
            dma((N, T)),
            dma((N, T)),
            pltpu.SemaphoreType.REGULAR,
            pltpu.SemaphoreType.REGULAR,
        ],
        compiler_params=pltpu.CompilerParams(collective_id=0, has_side_effects=True),
    )(x, in_gain[None], lw, rw, lg, rg, mid_gain[None], ow, og)
    out = out.reshape(parts, R // IT, S, IT, width).transpose(1, 3, 0, 2, 4)
    return out.reshape(R, C, width)


def solution(mesh):
    weight = P("trial", None)
    return jax.shard_map(
        functools.partial(local, mesh.shape["north"], mesh.shape["east"]),
        mesh=mesh,
        in_specs=(
            P(("trial", "north"), "east", None),
            P(), weight, weight, weight, weight, P(), weight, weight,
        ),
        out_specs=P(("trial", "north"), "east", None),
        check_vma=False,
    )
```

time: 16.9 us -> 13.4 us (0.79)
  Pallas kernels: 16.1 us -> 12.6 us
    pallas_call x1, Pallas kernels: 16.1 us -> 12.6 us  [local(): pl.pallas_call(functools.partial(kernel, (N, E, R, C, IT, JT)), out_shape...]
where the time goes in v3:
time: 13.4 us; the launch traced here: 13.3 us
  Pallas kernels  12.6 us (94%)
  local copies, waits for them, and re-layouts  0.64 us (5%)
    pallas_call x1, Pallas kernels, local(): pl.pallas_call(functools.partial(kernel, (N, E, R, C, IT, JT)), out_shape...  12.6 us
    unnamed x1, local copies, waits for them, and re-layouts  0.64 us

profile of v3, /device:TPU:0, one launch (start us, length us, event | category | flops | bytes accessed | tf_op | source)
XLA Modules:
  0.0 13.3 jit_solution(8463051940981508813)
XLA Ops:
  0.0 12.6 %shard_map.91 = bf16[288,128]{1,0:T(8,128)(2,1)S(1)} custom-call(bf16[288,128]{1,0:T(8,128)(2,1)} %bitcast.13, f32[1,128]{1,0:T(1,128)} %bitcast.14, bf16[128,128]{1,0:T(8,128)(2,1)} %lw_hbm.1, bf16[128,128]{1,0:T(8,128)(2,1)} %rw_hbm.1, bf16[128,128]{1,0:T(8,128)(2,1)} %lg_hbm.1, bf16[128,128]{1,0:T(8,128)(2,1)} %rg_hbm.1, f32[1,128]{1,0:T(1,128)} %bitcast.15, ...), custom_call_target="tpu_custom_call" | custom-call | tf_op jit(solution)/shard_map/pallas_call | solution.py:223
  12.6 0.6 %copy.12 = bf16[24,12,128]{2,0,1:T(8,128)(2,1)} copy(bf16[24,12,128]{2,0,1:T(8,128)(2,1)S(1)} %bitcast.12) | data formatting | bytes 147456

commit v4 on v3

--- a/solution.py
+++ b/solution.py
@@ -40,7 +40,7 @@
     x_hbm, in_gain_hbm, lw_hbm, rw_hbm, lg_hbm, rg_hbm, mid_gain_hbm, ow_hbm, og_hbm,
     out_ref,
     x, in_gain, lw, rw, lg, rg, mid_gain, ow, og,
-    left, right, gate, packed, pieces, sent, got, right_sent, right_got,
+    ready, left, right, gate, packed, pieces, sent, got, right_sent, right_got,
     load_sem, sent_sem, got_sem, right_sent_sem, right_got_sem, below_sem, above_sem,
 ):
     N, E, R, C, IT, JT = sizes
@@ -65,26 +65,25 @@
         pltpu.make_async_copy(src, dst, load_sem.at[at])
         for at, (src, dst) in enumerate(
             (
-                (x_hbm, x), (in_gain_hbm, in_gain), (lw_hbm, lw), (lg_hbm, lg), (rw_hbm, rw),
-                (rg_hbm, rg), (og_hbm, og), (mid_gain_hbm, mid_gain), (ow_hbm, ow),
+                (x_hbm, x), (in_gain_hbm, in_gain), (rw_hbm, rw), (rg_hbm, rg), (lw_hbm, lw),
+                (lg_hbm, lg), (og_hbm, og), (mid_gain_hbm, mid_gain), (ow_hbm, ow),
             )
         )
     ]
     for load in loads:
         load.start()
-    for load in loads:
+    for load in loads[:4]:
         load.wait()
 
-    def own(at):
+    def make_right(at):
         at_rows = pl.ds(pl.multiple_of(at * block, block), block)
-        ready = norm_channels(x[at_rows, :].astype(jnp.float32), in_gain[...]).astype(jnp.bfloat16)
-        right[at_rows, :] = dot(ready, rw[...]) * logistic(dot(ready, rg[...]))
-        left[at_rows, :] = dot(ready, lw[...]) * logistic(dot(ready, lg[...]))
-        gate[at_rows, :] = logistic(dot(ready, og[...]))
+        normed = norm_channels(x[at_rows, :].astype(jnp.float32), in_gain[...]).astype(jnp.bfloat16)
+        ready[at_rows, :] = normed
+        right[at_rows, :] = dot(normed, rw[...]) * logistic(dot(normed, rg[...]))
         if S == R:
             right_sent[0, at_rows, :] = right[at_rows, :].astype(jnp.bfloat16)
 
-    loop(rows // block, own)
+    loop(rows // block, make_right)
 
     if S < R:
         for t in range(T):
@@ -115,6 +114,20 @@
         signal(below_sem, "east", above)
         signal(above_sem, "east", below)
 
+    for load in loads[4:]:
+        load.wait()
+
+    def make_left(at):
+        at_rows = pl.ds(pl.multiple_of(at * block, block), block)
+        normed = ready[at_rows, :]
+        left[at_rows, :] = dot(normed, lw[...]) * logistic(dot(normed, lg[...]))
+
+    def make_gate(at):
+        at_rows = pl.ds(pl.multiple_of(at * block, block), block)
+        gate[at_rows, :] = logistic(dot(ready[at_rows, :], og[...]))
+
+    loop(rows // block, make_left)
+
     def tile(m, t, right_ref, stride, offset):
         def one(at):
             it, jt = at // (S // JT), at % (S // JT)
@@ -125,7 +138,7 @@
                 return tuple(sums[a] + lanes * right_ref[pl.ds(first + a, 1), :] for a in range(JT))
 
             zeros = jnp.zeros((IT, left.shape[1]), jnp.float32)
-            sums = lax.fori_loop(0, C, step, (zeros,) * JT, unroll=2)
+            sums = lax.fori_loop(0, C, step, (zeros,) * JT, unroll=4)
             at_rows = pl.ds(pl.multiple_of(at * block, block), block)
             sent[m, t, at_rows, :] = jnp.concatenate(sums, axis=0).astype(jnp.bfloat16)
 
@@ -161,6 +174,7 @@
 
     send(n, lambda copy: copy.start())
 
+    loop(rows // block, make_gate)
     for d in range(1, N):
         m = lax.rem(n + N - d, N)
         for t in range(T):
@@ -235,6 +249,7 @@
             pltpu.VMEM((1, mix), f32),
             pltpu.VMEM((mix, width), bf16),
             pltpu.VMEM((width, width), bf16),
+            pltpu.VMEM((rows, width), bf16),
             pltpu.VMEM((rows, mix), f32),
             pltpu.VMEM((rows, mix), f32),
             pltpu.VMEM((rows, width), f32),

time: 13.4 us -> 13.5 us (level)
  no operation moved by 1% of the time
where the time goes in v4:
time: 13.5 us; the launch traced here: 13.3 us
  Pallas kernels  12.7 us (94%)
  local copies, waits for them, and re-layouts  0.64 us (5%)
    pallas_call x1, Pallas kernels, local(): pl.pallas_call(functools.partial(kernel, (N, E, R, C, IT, JT)), out_shape...  12.7 us
    unnamed x1, local copies, waits for them, and re-layouts  0.64 us

profile of v4, /device:TPU:0, one launch (start us, length us, event | category | flops | bytes accessed | tf_op | source)
XLA Modules:
  0.0 13.3 jit_solution(17278329031492376977)
XLA Ops:
  0.0 12.7 %shard_map.91 = bf16[288,128]{1,0:T(8,128)(2,1)S(1)} custom-call(bf16[288,128]{1,0:T(8,128)(2,1)} %bitcast.13, f32[1,128]{1,0:T(1,128)} %bitcast.14, bf16[128,128]{1,0:T(8,128)(2,1)} %lw_hbm.1, bf16[128,128]{1,0:T(8,128)(2,1)} %rw_hbm.1, bf16[128,128]{1,0:T(8,128)(2,1)} %lg_hbm.1, bf16[128,128]{1,0:T(8,128)(2,1)} %rg_hbm.1, f32[1,128]{1,0:T(1,128)} %bitcast.15, ...), custom_call_target="tpu_custom_call" | custom-call | tf_op jit(solution)/shard_map/pallas_call | solution.py:237
  12.7 0.6 %copy.12 = bf16[24,12,128]{2,0,1:T(8,128)(2,1)} copy(bf16[24,12,128]{2,0,1:T(8,128)(2,1)S(1)} %bitcast.12) | data formatting | bytes 147456
